TPU v7x, 32 devices: a whole 2x2x4 slice. The times are simulated.
32 devices in a mesh: slab: 8 (over z, y), sub: 4 (over x, core).
Axes of the slice: x: 2, y: 2, z: 4, core: 2. Of those that a mesh axis runs over, the one named last changes fastest.
Arguments:
- factor_obs: float32 [32, 64, 64, 512], P('slab', 'sub'), may hold values from -0.20992233 to 0.20992233
- factor_ctrl: float32 [32, 64, 64, 512], P('slab', 'sub'), may hold values from -0.20992233 to 0.20992233
- diffusivity: float32 [32, 4096], P('slab', 'sub'), may hold values from 0.5 to 2
- input_map: float32 [4, 32, 4096], P(None, 'slab', 'sub'), may hold values from -2 to 2
- output_map: float32 [4, 32, 4096], P(None, 'slab', 'sub'), may hold values from -2 to 2
- start_block: float32 [512, 128], replicated, may hold values from -6 to 6
- order: int32 [1], replicated, may hold values from 64 to 128
Outputs:
- reduced_mass: float32 [128, 128], replicated
- reduced_state: float32 [128, 128], replicated
- reduced_input: float32 [128, 4], replicated
- reduced_output: float32 [4, 128], replicated
All inputs are finite; a program needn't handle non-finite values.
Results may differ from a plain program's by a relative error of at most 0.00017.
Values sent between devices are 32-bit elements; how exact they have to be, the bound alone decides.
A program may use at most 128 MiB of HBM per device.

v0:
```python
import jax
import jax.numpy as jnp
from jax import lax
from jax.sharding import PartitionSpec as P


def padded_2(cells, sides, width):
    for axis, dim in sides:
        count = lax.axis_size(axis)
        ends = count - 1
        head = lax.slice_in_dim(cells, 0, width, axis=dim)
        tail = lax.slice_in_dim(cells, cells.shape[dim] - width, cells.shape[dim], axis=dim)
        cells = jnp.concatenate(
            [
                lax.ppermute(tail, axis, [(i, (i + 1) % count) for i in range(ends)]),
                cells,
                lax.ppermute(head, axis, [((i + 1) % count, i) for i in range(ends)]),
            ],
            axis=dim,
        )
    return cells


def matmul(first, second):
    return jnp.dot(
        first, second, precision=lax.Precision.HIGHEST, preferred_element_type=jnp.float32
    )


def contract_cells(first, second):
    return lax.dot_general(
        first,
        second,
        (((0,), (0,)), ((), ())),
        precision=lax.Precision.HIGHEST,
        preferred_element_type=jnp.float32,
    )


def orthonormal(start):
    gram = matmul(start.T, start)
    lower_factor = jnp.linalg.cholesky(gram)
    return lax.linalg.triangular_solve(
        lower_factor, start, left_side=False, lower=True, transpose_a=True
    )


def subspace_bases(cross_gram, start_block):
    right_basis = orthonormal(matmul(cross_gram.T, start_block))
    left_basis = orthonormal(matmul(cross_gram, right_basis))
    right_basis = orthonormal(matmul(cross_gram.T, left_basis))
    left_basis = orthonormal(matmul(cross_gram, right_basis))
    return (left_basis, right_basis)


def stencil_padded(padded, conduct):
    center = padded[1:-1, 1:-1]
    beside = padded[2:, 1:-1] + padded[:-2, 1:-1] + padded[1:-1, 2:] + padded[1:-1, :-2]
    along = jnp.pad(center, ((0, 0), (0, 0), (1, 1), (0, 0)))
    beside = beside + along[:, :, 2:] + along[:, :, :-2]
    return conduct[..., None] * (beside - 6.0 * center) / 6.0


def on_device(factor_obs, factor_ctrl, diffusivity, input_map, output_map, start_block, order):
    plane_count, line_count, point_count, rank_count = factor_ctrl.shape
    cell_count = plane_count * line_count * point_count
    observe = factor_obs.reshape(cell_count, rank_count)
    control = factor_ctrl.reshape(cell_count, rank_count)
    conduct = diffusivity.reshape(plane_count, line_count, point_count)
    drive = input_map.reshape(input_map.shape[0], cell_count)
    sense = output_map.reshape(output_map.shape[0], cell_count)
    basis_count = start_block.shape[1]
    cross_gram = lax.psum(contract_cells(observe, control), ("slab", "sub"))
    factor_padded = padded_2(factor_ctrl, (("slab", 0), ("sub", 1)), 1)
    left_basis, right_basis = subspace_bases(cross_gram, start_block)
    projected = matmul(factor_padded.reshape(-1, rank_count), right_basis).reshape(
        plane_count + 2, line_count + 2, point_count, basis_count
    )
    ctrl_space = projected[1:-1, 1:-1].reshape(cell_count, basis_count)
    applied = stencil_padded(projected, conduct).reshape(cell_count, basis_count)
    obs_space = matmul(observe, left_basis)
    state_small, input_rows, output_small = lax.psum(
        (contract_cells(obs_space, applied), matmul(drive, obs_space), matmul(sense, ctrl_space)),
        ("slab", "sub"),
    )
    input_small = input_rows.T
    kept_mask = (jnp.arange(basis_count, dtype=jnp.int32) < order[0]).astype(jnp.float32)
    square_mask = kept_mask[:, None] * kept_mask[None, :]
    reduced_mass = square_mask * matmul(left_basis.T, matmul(cross_gram, right_basis))
    reduced_state = square_mask * state_small
    reduced_input = kept_mask[:, None] * input_small
    reduced_output = kept_mask[None, :] * output_small
    return (reduced_mass, reduced_state, reduced_input, reduced_output)


def solution(mesh):
    placed = (
        P("slab", "sub", None, None),
        P("slab", "sub", None, None),
        P("slab", "sub"),
        P(None, "slab", "sub"),
        P(None, "slab", "sub"),
        P(),
        P(),
    )
    return jax.shard_map(
        on_device, mesh=mesh, in_specs=placed, out_specs=(P(), P(), P(), P()), check_vma=False
    )
```

profile of v0, /device:TPU:0, one launch (start us, length us, event | category | flops | bytes accessed | tf_op | source)
XLA Modules:
  0.0 465.0 jit_solution(2008871766227018327)
XLA Ops:
  7.2 0.0 copy-start
  7.2 0.0 all-reduce.5.cloned.1.call-start
  7.2 17.3 %convolution_bitcast_fusion = f32[512,512]{1,0:T(8,128)} fusion(f32[4,16,64,512]{3,2,1,0:T(8,128)} %param.10, f32[4,16,64,512]{3,2,1,0:T(8,128)} %param.11), kind=kOutput, calls=%fused_computation.16 | convolution fusion | flops 12884901888 | bytes 17825792 | tf_op jit(solution)/shard_map/dot_general | solution.py:31
  24.5 0.0 all-reduce.5.cloned.1.call-update
  24.5 0.0 copy-start.3
  24.6 0.0 all-reduce.7.cloned.1.call-start
  24.6 5.1 %fusion.35 = (f32[1,16,64,512]{3,2,1,0:T(8,128)}, f32[1,16,64,512]{3,2,1,0:T(8,128)}) fusion(f32[4,16,64,512]{3,2,1,0:T(8,128)} %param.11), kind=kLoop, calls=%fused_computation.69 | loop fusion | bytes 8388608 | tf_op jit(solution)/shard_map/slice | solution.py:11
  29.7 6.2 %collective-permute-start = (f32[1,16,64,512]{3,2,1,0:T(8,128)}, f32[1,16,64,512]{3,2,1,0:T(8,128)}, u32[]{:S(2)}, u32[]{:S(2)}) collective-permute-start(f32[1,16,64,512]{3,2,1,0:T(8,128)} %get-tuple-element.11), channel_id=1, source_target_pairs={{0,4},{4,8},{8,12},{12,16},{16,20},{20,24},{24,28},{1,5},{5,9},{9,... | collective-permute-start | bytes 6291464 | tf_op jit(solution)/shard_map/ppermute | solution.py:15
  35.9 1.7 collective-permute-start.1
  38.5 0.1 mul.53
  38.5 144.2 %all-reduce.5.cloned.1.call-done = f32[512,512]{1,0:T(8,128)} async-done(((f32[512,512]{1,0:T(8,128)}), f32[512,512]{1,0:T(8,128)}) %all-reduce.5.cloned.1.call-update) | async-done | bytes 1048592 | tf_op jit(solution)/shard_map/psum | solution.py:73
  182.8 3.1 fusion.36
  185.9 0.6 fusion.37
  186.5 0.1 copy.11
  186.6 11.7 %cholesky.74 = f32[128,128]{1,0:T(8,128)S(1)} custom-call(f32[128,128]{1,0:T(8,128)S(1)} %fusion.26), custom_call_target="Cholesky" | custom-call | tf_op jit(solution)/shard_map/jit(cholesky)/cholesky | solution.py:42
  198.3 0.6 compare_reduce_fusion.3
  199.0 0.7 fusion.14
  199.7 9.8 %custom-call.8 = f32[1,128,128]{1,2,0:T(8,128)S(1)} custom-call(f32[1,128,128]{2,1,0:T(8,128)S(1)} %fusion.14), custom_call_target="InvertDiagBlocksLowerTriangular" | custom-call | tf_op jit(solution)/shard_map/triangular_solve/custom-call.0 | solution.py:43
  209.5 0.4 convolution_bitcast_fusion.3
  209.9 1.0 fusion.38
  210.9 0.6 fusion.39
  211.5 0.1 copy.12
  211.6 11.9 %cholesky.85 = f32[128,128]{1,0:T(8,128)S(1)} custom-call(f32[128,128]{1,0:T(8,128)S(1)} %fusion.24), custom_call_target="Cholesky" | custom-call | tf_op jit(solution)/shard_map/jit(cholesky)/cholesky | solution.py:42
  223.5 0.6 compare_reduce_fusion.2
  224.1 0.7 fusion.15
  224.8 9.8 %custom-call.9 = f32[1,128,128]{1,2,0:T(8,128)S(1)} custom-call(f32[1,128,128]{2,1,0:T(8,128)S(1)} %fusion.15), custom_call_target="InvertDiagBlocksLowerTriangular" | custom-call | tf_op jit(solution)/shard_map/triangular_solve/custom-call.0 | solution.py:43
  234.6 0.4 convolution_bitcast_fusion.2
  235.0 1.8 fusion.40
  236.9 0.6 fusion.41
  237.5 0.1 copy.13
  237.6 11.7 %cholesky.96 = f32[128,128]{1,0:T(8,128)S(1)} custom-call(f32[128,128]{1,0:T(8,128)S(1)} %fusion.22), custom_call_target="Cholesky" | custom-call | tf_op jit(solution)/shard_map/jit(cholesky)/cholesky | solution.py:42
  249.3 0.6 compare_reduce_fusion.1
  250.0 0.7 fusion.16
  250.6 10.0 %custom-call.10 = f32[1,128,128]{1,2,0:T(8,128)S(1)} custom-call(f32[1,128,128]{2,1,0:T(8,128)S(1)} %fusion.16), custom_call_target="InvertDiagBlocksLowerTriangular" | custom-call | tf_op jit(solution)/shard_map/triangular_solve/custom-call.0 | solution.py:43
  260.6 0.4 fusion.20
  261.1 1.0 fusion.12
  262.1 0.6 fusion.42
  262.6 0.1 copy.14
  262.8 11.7 %cholesky.107 = f32[128,128]{1,0:T(8,128)S(1)} custom-call(f32[128,128]{1,0:T(8,128)S(1)} %fusion.19), custom_call_target="Cholesky" | custom-call | tf_op jit(solution)/shard_map/jit(cholesky)/cholesky | solution.py:42
  274.5 0.6 compare_reduce_fusion
  275.2 0.7 fusion.17
  275.8 9.8 %custom-call.11 = f32[1,128,128]{1,2,0:T(8,128)S(1)} custom-call(f32[1,128,128]{2,1,0:T(8,128)S(1)} %fusion.17), custom_call_target="InvertDiagBlocksLowerTriangular" | custom-call | tf_op jit(solution)/shard_map/triangular_solve/custom-call.0 | solution.py:43
  285.6 0.4 convolution_bitcast_fusion.1
  286.1 0.0 slice-start
  286.1 3.3 constant_dynamic-update-slice_fusion.2
  289.4 8.7 %constant_dynamic-update-slice_fusion.1 = f32[6,16,64,512]{3,2,1,0:T(8,128)} fusion(f32[6,16,64,512]{3,2,1,0:T(8,128)} %constant_dynamic-update-slice_fusion.2, f32[4,16,64,512]{3,2,1,0:T(8,128)} %param.11), kind=kLoop, calls=%fused_computation.58 | loop fusion | bytes 16777216
  298.1 3.1 constant_dynamic-update-slice_fusion
  301.2 1.5 fusion.34
  302.8 1.3 collective-permute-start.2
  304.1 1.7 collective-permute-start.3
  305.8 1.0 convolution_multiply_fusion
  306.8 8.7 %fusion.43 = f32[128,4096]{1,0:T(8,128)S(1)} fusion(f32[512,128]{0,1:T(8,128)S(1)} %convolution_bitcast_fusion.1, f32[4096,512]{1,0:T(8,128)S(1)} %bitcast.101), kind=kOutput, calls=%fused_computation.77 | convolution fusion | flops 3221225472 | bytes 10747904 | tf_op jit(solution)/shard_map/dot_general | solution.py:25
  315.5 1.7 convolution_bitcast_fusion.5
  317.2 0.0 collective-permute-done.3
  317.3 12.6 %fusion = f32[6,18,64,128]{3,2,1,0:T(8,128)S(1)} fusion(f32[6,1,64,512]{3,2,1,0:T(8,128)S(1)} %collective-permute-done.3, f32[6,16,64,512]{3,2,1,0:T(8,128)S(1)} %copy-done.2, f32[6,1,64,512]{3,2,1,0:T(8,128)S(1)} %collective-permute-done.2, f32[128,512]{1,0:T(8,128)S(1)} %fusion.20), kind=kOutput, calls=%fused_computation | convolution fusion | flops 5442895872 | bytes 17956864 | tf_op jit(solution)/shard_map/dot_general | solution.py:25
  329.9 0.2 slice.57
  330.1 1.9 fusion.10
  332.1 2.8 fusion.44
  334.9 0.0 all-reduce.7.cloned.1.call-update
  334.9 1.2 convolution_bitcast_fusion.4
  336.1 42.1 %all-reduce.1 = (f32[4,128]{1,0:T(4,128)S(1)}, f32[4,128]{1,0:T(4,128)S(1)}) all-reduce(f32[4,128]{1,0:T(4,128)S(1)} %convolution_bitcast_fusion.5, f32[4,128]{1,0:T(4,128)S(1)} %convolution_bitcast_fusion.4), channel_id=1, replica_groups=mesh['slab'=8,'sub'=4] {'slab','sub'}, use_global_device_ids=true, to_apply=%region_4.7 | all-reduce | flops 1024 | bytes 8192 | tf_op jit(solution)/shard_map/psum | solution.py:82
  378.2 0.6 broadcast_multiply_fusion
  378.8 77.6 %all-reduce.7.cloned.1.call-done = f32[128,128]{1,0:T(8,128)} async-done(((f32[128,128]{1,0:T(8,128)}), f32[128,128]{1,0:T(8,128)}) %all-reduce.7.cloned.1.call-update) | async-done | bytes 65552 | tf_op jit(solution)/shard_map/psum | solution.py:82
  456.4 1.6 multiply_multiply_fusion
  (28 shorter events, 0.3 us)
Async XLA Ops:
  7.2 175.6 %copy-start = (f32[512,128]{1,0:T(8,128)S(1)}, f32[512,128]{1,0:T(8,128)}, u32[]{:S(2)}) copy-start(f32[512,128]{1,0:T(8,128)} %param.15) | copy-start | bytes 786436
  7.2 175.6 %all-reduce.5.cloned.1.call-start = ((), (), s32[]{:S(2)}) async-start(), calls=%async_computation | async-start | bytes 2097152 | tf_op jit(solution)/shard_map/psum | solution.py:73
  24.5 13.1 %copy-start.3 = (f32[4,4,1024]{2,1,0:T(4,128)S(1)}, f32[4,4,1024]{2,1,0:T(4,128)}, u32[]{:S(2)}) copy-start(f32[4,4,1024]{2,1,0:T(4,128)} %param.14) | copy-start | bytes 196612
  24.5 13.2 %copy-start.4 = (f32[4,4,1024]{2,1,0:T(4,128)S(1)}, f32[4,4,1024]{2,1,0:T(4,128)}, u32[]{:S(2)}) copy-start(f32[4,4,1024]{2,1,0:T(4,128)} %param.13) | copy-start | bytes 196612
  24.6 13.9 %copy-start.5 = (f32[4,1024]{1,0:T(4,128)S(1)}, f32[4,1024]{1,0:T(4,128)}, u32[]{:S(2)}) copy-start(f32[4,1024]{1,0:T(4,128)} %param.12) | copy-start | bytes 49156
  24.6 431.8 %all-reduce.7.cloned.1.call-start = ((), (), s32[]{:S(2)}) async-start(), calls=%async_computation.1 | async-start | bytes 131072 | tf_op jit(solution)/shard_map/psum | solution.py:82
  29.7 256.4 %collective-permute-start = (f32[1,16,64,512]{3,2,1,0:T(8,128)}, f32[1,16,64,512]{3,2,1,0:T(8,128)}, u32[]{:S(2)}, u32[]{:S(2)}) collective-permute-start(f32[1,16,64,512]{3,2,1,0:T(8,128)} %get-tuple-element.11), channel_id=1, source_target_pairs={{0,4},{4,8},{8,12},{12,16},{16,20},{20,24},{24,28},{1,5},{5,9},{9,... | collective-permute-start | bytes 6291464 | tf_op jit(solution)/shard_map/ppermute | solution.py:15
  35.9 262.2 %collective-permute-start.1 = (f32[1,16,64,512]{3,2,1,0:T(8,128)}, f32[1,16,64,512]{3,2,1,0:T(8,128)}, u32[]{:S(2)}, u32[]{:S(2)}) collective-permute-start(f32[1,16,64,512]{3,2,1,0:T(8,128)} %get-tuple-element.10), channel_id=1, source_target_pairs={{4,0},{8,4},{12,8},{16,12},{20,16},{24,20},{28,24},{5,1},{9,5},{13... | collective-permute-start | bytes 6291464 | tf_op jit(solution)/shard_map/ppermute | solution.py:17
  182.8 27.1 %copy-start.1 = (f32[512,512]{1,0:T(8,128)S(1)}, f32[512,512]{1,0:T(8,128)}, u32[]{:S(2)}) copy-start(f32[512,512]{1,0:T(8,128)} %all-reduce.5.cloned.1.call-done) | copy-start | bytes 3145732
  286.1 20.8 %slice-start = ((s8[8388608]{0:T(1024)(128)(4,1)}), s8[4194304]{0:T(1024)(128)(4,1)S(1)}, s32[]{:S(2)}) async-start(s8[8388608]{0:T(1024)(128)(4,1)} %bitcast.99), calls=%async_computation.2 | async-start | bytes 8388608
  289.4 17.4 %slice-start.1 = ((s8[8388608]{0:T(1024)(128)(4,1)}), s8[4194304]{0:T(1024)(128)(4,1)S(1)}, s32[]{:S(2)}) async-start(s8[8388608]{0:T(1024)(128)(4,1)} %bitcast.99), calls=%async_computation.3 | async-start | bytes 8388608
  302.8 14.5 %collective-permute-start.2 = (f32[6,1,64,512]{3,2,1,0:T(8,128)S(1)}, f32[6,1,64,512]{3,2,1,0:T(8,128)S(1)}, u32[]{:S(2)}, u32[]{:S(2)}) collective-permute-start(f32[6,1,64,512]{3,2,1,0:T(8,128)S(1)} %get-tuple-element.8), channel_id=1, source_target_pairs={{0,1},{1,2},{2,3},{4,5},{5,6},{6,7},{8,9},{9,10},{10,11},{12,13},{... | collective-permute-start | bytes 2359304 | tf_op jit(solution)/shard_map/ppermute | solution.py:15
  304.1 13.2 %collective-permute-start.3 = (f32[6,1,64,512]{3,2,1,0:T(8,128)S(1)}, f32[6,1,64,512]{3,2,1,0:T(8,128)S(1)}, u32[]{:S(2)}, u32[]{:S(2)}) collective-permute-start(f32[6,1,64,512]{3,2,1,0:T(8,128)S(1)} %get-tuple-element.9), channel_id=1, source_target_pairs={{1,0},{2,1},{3,2},{5,4},{6,5},{7,6},{9,8},{10,9},{11,10},{13,12},{... | collective-permute-start | bytes 2359304 | tf_op jit(solution)/shard_map/ppermute | solution.py:17
  306.8 10.4 %copy-start.2 = (f32[6,16,64,512]{3,2,1,0:T(8,128)S(1)}, f32[6,16,64,512]{3,2,1,0:T(8,128)}, u32[]{:S(2)}) copy-start(f32[6,16,64,512]{3,2,1,0:T(8,128)} %constant_dynamic-update-slice_fusion) | copy-start | bytes 37748740
Sparse Core Ops, SparseCore 0:
  24.7 158.0 all-reduce.4
  335.0 121.3 all-reduce.6
where the time goes:
time: 470 us; the launch traced here: 465 us
  waiting for transfers between devices  222 us (47%)
  other arithmetic  95.9 us (20%)
  matrix products  56.2 us (12%)
  blocking collectives  42.1 us (9%)
  local copies, waits for them, and re-layouts  22.5 us (5%)
  between operations  15.3 us (3%)
  starting transfers between devices  11.1 us (2%)
    psum x1, waiting for transfers between devices, on_device(): cross_gram = lax.psum(contract_cells(observe, control), ('slab', 'sub'))  144 us
    psum x1, waiting for transfers between devices, on_device(): lax.psum((contract_cells(obs_space, applied), matmul(drive, obs_space), m...  77.6 us
    another operation x12, other arithmetic, orthonormal(): lower_factor = jnp.linalg.cholesky(gram)  49.7 us
    psum x1, blocking collectives, on_device(): lax.psum((contract_cells(obs_space, applied), matmul(drive, obs_space), m...  42.1 us
    another operation x8, other arithmetic, orthonormal(): lax.linalg.triangular_solve(lower_factor, start, left_side=False, lower=T...  42 us
    dot_general x13, matrix products, matmul(): jnp.dot(first, second, precision=lax.Precision.HIGHEST, preferred_element...  34.5 us
    dot_general x2, matrix products, contract_cells(): lax.dot_general(first, second, (((0,), (0,)), ((), ())), precision=lax.Pr...  20.1 us
    unnamed x20, local copies, waits for them, and re-layouts  12.2 us
  transfers between devices with their start and end apart: 6, of which 2 were waited for; matrix products, arithmetic and copies ran while one was open for 29% of the time, Pallas kernels for 0%

commit v1 on v0

v1 whole, which is shorter than its diff:
```python
import functools
import jax
import jax.numpy as jnp
from jax import lax
from jax.experimental import pallas as pl
from jax.experimental.pallas import tpu as pltpu
from jax.sharding import PartitionSpec as P

LANES = 128
PANEL = 8
HIGHEST = lax.Precision.HIGHEST
HIGH = lax.Precision.HIGH


def exact(first, second, dims=((1,), (0,))):
    return lax.dot_general(
        first, second, (dims, ((), ())), precision=HIGHEST, preferred_element_type=jnp.float32
    )


def tall(first, second, dims=((1,), (0,))):
    return lax.dot_general(
        first, second, (dims, ((), ())), precision=HIGH, preferred_element_type=jnp.float32
    )


def sub_bits(count):
    return [1 << b for b in range(count.bit_length() - 1)]


def all_reduce_kernel(nslab, nsub, in_ref, out_ref, work, got_sub, got_slab, *sems):
    rs_sub_send, rs_sub_recv, rs_slab_send, rs_slab_recv = sems[:4]
    ag_slab_send, ag_slab_recv, ag_sub_send, ag_sub_recv = sems[4:]
    slab, sub = lax.axis_index("slab"), lax.axis_index("sub")
    rows, cols = work.shape[0], in_ref.shape[1]
    bits = sub_bits(nsub)

    def partner(bit):
        has = lax.rem(sub // bit, 2)
        return has, sub + bit - 2 * bit * has

    barrier = pltpu.get_barrier_semaphore()
    for bit in bits:
        pl.semaphore_signal(barrier, inc=1, device_id={"sub": partner(bit)[1]})
    for off in range(1, nslab):
        pl.semaphore_signal(barrier, inc=1, device_id={"slab": lax.rem(slab + off, nslab)})

    tall_rows = in_ref.shape[0]
    for c in range(cols // LANES):
        work[c * tall_rows : (c + 1) * tall_rows, :] = in_ref[:, c * LANES : (c + 1) * LANES]
    pl.semaphore_wait(barrier, len(bits) + nslab - 1)

    base, length, taken = 0, rows, 0
    for s, bit in enumerate(bits):
        half = length // 2
        has, other = partner(bit)
        keep = pl.multiple_of(base + has * half, 8)
        give = pl.multiple_of(base + (1 - has) * half, 8)
        copy = pltpu.make_async_remote_copy(
            src_ref=work.at[pl.ds(give, half)],
            dst_ref=got_sub.at[pl.ds(taken, half)],
            send_sem=rs_sub_send.at[s],
            recv_sem=rs_sub_recv.at[s],
            device_id={"sub": other},
        )
        copy.start()
        copy.wait()
        work[pl.ds(keep, half), :] += got_sub[taken : taken + half, :]
        base, length, taken = keep, half, taken + half

    piece = length // nslab
    copies = []
    for off in range(1, nslab):
        peer = lax.rem(slab + off, nslab)
        copy = pltpu.make_async_remote_copy(
            src_ref=work.at[pl.ds(pl.multiple_of(base + peer * piece, 8), piece)],
            dst_ref=got_slab.at[off],
            send_sem=rs_slab_send.at[off],
            recv_sem=rs_slab_recv.at[off],
            device_id={"slab": peer},
        )
        copy.start()
        copies.append(copy)
    mine = pl.multiple_of(base + slab * piece, 8)
    total = work[pl.ds(mine, piece), :]
    for off in range(1, nslab):
        copies[off - 1].wait_recv()
        total = total + got_slab[off]
    out_ref[pl.ds(mine, piece), :] = total
    for copy in copies:
        copy.wait_send()

    copies = []
    for off in range(1, nslab):
        copy = pltpu.make_async_remote_copy(
            src_ref=out_ref.at[pl.ds(mine, piece)],
            dst_ref=out_ref.at[pl.ds(mine, piece)],
            send_sem=ag_slab_send.at[off],
            recv_sem=ag_slab_recv.at[off],
            device_id={"slab": lax.rem(slab + off, nslab)},
        )
        copy.start()
        copies.append(copy)
    for copy in copies:
        copy.wait()

    for s in reversed(range(len(bits))):
        has, other = partner(bits[s])
        copy = pltpu.make_async_remote_copy(
            src_ref=out_ref.at[pl.ds(base, length)],
            dst_ref=out_ref.at[pl.ds(base, length)],
            send_sem=ag_sub_send.at[s],
            recv_sem=ag_sub_recv.at[s],
            device_id={"sub": other},
        )
        copy.start()
        copy.wait()
        base = pl.multiple_of(base - has * length, 8)
        length = 2 * length


def all_reduce(part, ident):
    nslab, nsub = lax.axis_size("slab"), lax.axis_size("sub")
    rows = part.shape[0] * (part.shape[1] // LANES)
    bits = len(sub_bits(nsub))
    piece = rows // (nsub * nslab)
    sub_sem, slab_sem = pltpu.SemaphoreType.DMA((bits,)), pltpu.SemaphoreType.DMA((nslab,))
    return pl.pallas_call(
        functools.partial(all_reduce_kernel, nslab, nsub),
        out_shape=jax.ShapeDtypeStruct((rows, LANES), jnp.float32),
        in_specs=[pl.BlockSpec(memory_space=pltpu.VMEM)],
        out_specs=pl.BlockSpec(memory_space=pltpu.VMEM),
        scratch_shapes=[
            pltpu.VMEM((rows, LANES), jnp.float32),
            pltpu.VMEM((rows, LANES), jnp.float32),
            pltpu.VMEM((nslab, piece, LANES), jnp.float32),
            sub_sem, sub_sem, slab_sem, slab_sem, slab_sem, slab_sem, sub_sem, sub_sem,
        ],
        compiler_params=pltpu.CompilerParams(collective_id=ident, has_side_effects=True),
    )(part)


def inverse_factor(work, size):
    for base in range(0, size, PANEL):
        rows = [
            jnp.broadcast_to(work[base + i : base + i + 1, :], (PANEL, 2 * size))
            for i in range(PANEL)
        ]
        block = [
            [
                jnp.broadcast_to(rows[i][:, base + j : base + j + 1], (PANEL, LANES))
                if j >= i
                else None
                for j in range(PANEL)
            ]
            for i in range(PANEL)
        ]
        wide = 2 * size // LANES
        for j in range(PANEL):
            scale = lax.rsqrt(block[j][j])
            lead = [block[j][i] * scale if i > j else None for i in range(PANEL)]
            rows[j] = rows[j] * jnp.concatenate([scale] * wide, axis=1)
            for i in range(j + 1, PANEL):
                for m in range(i, PANEL):
                    block[i][m] = block[i][m] - lead[i] * lead[m]
                rows[i] = rows[i] - jnp.concatenate([lead[i]] * wide, axis=1) * rows[j]
        place = lax.broadcasted_iota(jnp.int32, (PANEL, 2 * size), 0)
        panel = rows[0]
        for i in range(1, PANEL):
            panel = jnp.where(place == i, rows[i], panel)
        work[base : base + PANEL, :] = panel
        if base + PANEL < size:
            left = panel[:, :size]
            update = exact(left, panel, ((0,), (0,)))
            work[base + PANEL :, :] = work[base + PANEL :, :] - update[base + PANEL :, :]


def bases_kernel(sweeps, gram_ref, start_ref, left_ref, right_ref, mass_ref, both, block, work):
    rank, size = start_ref.shape
    for c in range(rank // LANES):
        cols = slice(c * LANES, (c + 1) * LANES)
        tile = gram_ref[c * rank : (c + 1) * rank, :]
        both[1, :, cols] = tile
        both[0, cols, :] = tile.T
    block[...] = start_ref[...]
    row = lax.broadcasted_iota(jnp.int32, (size, size), 0)
    col = lax.broadcasted_iota(jnp.int32, (size, size), 1)
    eye = (row == col).astype(jnp.float32)

    def step(k, carry):
        product = exact(both[lax.rem(k, 2)], block[...])
        work[:, :size] = exact(product, product, ((0,), (0,)))
        work[:, size:] = eye
        inverse_factor(work, size)
        right_ref[...] = left_ref[...]
        basis = exact(product, work[:, size:], ((1,), (1,)))
        block[...] = basis
        left_ref[...] = basis
        return carry

    left_ref[...] = start_ref[...]
    lax.fori_loop(0, 2 * sweeps, step, 0)
    mass_ref[...] = exact(left_ref[...], exact(both[1], right_ref[...]), ((0,), (0,)))


def subspace_bases(cross_gram, start_block):
    rank, size = start_block.shape
    tall_shape = jax.ShapeDtypeStruct((rank, size), jnp.float32)
    vmem = pl.BlockSpec(memory_space=pltpu.VMEM)
    return pl.pallas_call(
        functools.partial(bases_kernel, 2),
        out_shape=(tall_shape, tall_shape, jax.ShapeDtypeStruct((size, size), jnp.float32)),
        in_specs=[vmem, vmem],
        out_specs=(vmem, vmem, vmem),
        scratch_shapes=[
            pltpu.VMEM((2, rank, rank), jnp.float32),
            pltpu.VMEM((rank, size), jnp.float32),
            pltpu.VMEM((size, 2 * size), jnp.float32),
        ],
    )(cross_gram, start_block)


def shifted(face, axis, step):
    count = lax.axis_size(axis)
    pairs = [(i, i + step) for i in range(count) if 0 <= i + step < count]
    return lax.ppermute(face, axis, pairs)


def on_device(factor_obs, factor_ctrl, diffusivity, input_map, output_map, start_block, order):
    planes, lines, points, rank = factor_ctrl.shape
    cells = planes * lines * points
    size = start_block.shape[1]
    observe = factor_obs.reshape(cells, rank)
    control = factor_ctrl.reshape(cells, rank)
    conduct = diffusivity.reshape(planes, lines, points)
    drive = input_map.reshape(input_map.shape[0], cells)
    sense = output_map.reshape(output_map.shape[0], cells)
    ins, outs = drive.shape[0], sense.shape[0]

    cross_gram = all_reduce(tall(observe, control, ((0,), (0,))), 0)
    left_basis, right_basis, mass = subspace_bases(cross_gram, start_block)

    ctrl_flat = tall(control, right_basis)
    ctrl = ctrl_flat.reshape(planes, lines, points, size)
    below = shifted(ctrl[-1:], "slab", 1)
    above = shifted(ctrl[:1], "slab", -1)
    before = shifted(ctrl[:, -1:], "sub", 1)
    after = shifted(ctrl[:, :1], "sub", -1)
    obs_space = tall(observe, left_basis)
    zs = jnp.concatenate([below, ctrl, above], axis=0)
    ys = jnp.concatenate([before, ctrl, after], axis=1)
    xs = jnp.pad(ctrl, ((0, 0), (0, 0), (1, 1), (0, 0)))
    beside = zs[2:] + zs[:-2] + ys[:, 2:] + ys[:, :-2] + xs[:, :, 2:] + xs[:, :, :-2]
    applied = (conduct[..., None] * (beside - 6.0 * ctrl) / 6.0).reshape(cells, size)
    state = tall(obs_space, applied, ((0,), (0,)))
    used = size + ins + outs
    grain = 8 * lax.axis_size("slab") * lax.axis_size("sub")
    packed = jnp.concatenate(
        [
            state,
            tall(drive, obs_space),
            tall(sense, ctrl_flat),
            jnp.zeros((-used % grain, size), jnp.float32),
        ],
        axis=0,
    )
    summed = all_reduce(packed, 1)
    kept = (jnp.arange(size, dtype=jnp.int32) < order[0]).astype(jnp.float32)
    square = kept[:, None] * kept[None, :]
    reduced_input = kept[:, None] * summed[size : size + ins].T
    reduced_output = kept[None, :] * summed[size + ins : used]
    return (square * mass, square * summed[:size], reduced_input, reduced_output)


def solution(mesh):
    placed = (
        P("slab", "sub", None, None),
        P("slab", "sub", None, None),
        P("slab", "sub"),
        P(None, "slab", "sub"),
        P(None, "slab", "sub"),
        P(),
        P(),
    )
    return jax.shard_map(
        on_device, mesh=mesh, in_specs=placed, out_specs=(P(), P(), P(), P()), check_vma=False
    )
```

time: 470 us -> 182 us (0.39)
  waiting for transfers between devices: 222 us -> 8.7 us
  Pallas kernels: 0 us -> 110 us
  other arithmetic: 95.9 us -> 6.94 us
  blocking collectives: 42.1 us -> 0 us
  matrix products: 56.2 us -> 37.8 us
  local copies, waits for them, and re-layouts: 22.5 us -> 6.27 us
  between operations: 15.3 us -> 1.47 us
    psum x2 -> x0, waiting for transfers between devices: 222 us -> none  [the longest x1 144 us: on_device(): cross_gram = lax.psum(contract_cells(observe, control), ('slab', 'sub'))]
    pallas_call x0 -> x3, Pallas kernels: none -> 110 us  [the longest x2 62.9 us: all_reduce(): pl.pallas_call(functools.partial(all_reduce_kernel, nslab, nsub), out_sha...]
    another operation x20 -> x0, other arithmetic: 91.7 us -> none  [the longest x12 49.7 us: orthonormal(): lower_factor = jnp.linalg.cholesky(gram)]
    psum x1 -> x0, blocking collectives: 42.1 us -> none  [on_device(): lax.psum((contract_cells(obs_space, applied), matmul(drive, obs_space), m...]
    dot_general x15 -> x6, matrix products: 54.5 us -> 37.8 us  [tall(): lax.dot_general(first, second, (dims, ((), ())), precision=HIGH, preferre...]
    unnamed x20 -> x16, local copies, waits for them, and re-layouts: 12.2 us -> 1.27 us
    ppermute x4, waiting for transfers between devices: 0.02 us -> 8.7 us  [shifted(): return lax.ppermute(face, axis, pairs)]
  transfers between devices with their start and end apart: 6 -> 4, of which waited for: 2 -> 1; matrix products, arithmetic and copies ran while one was open for 29% -> 7% of each run, Pallas kernels for 0% -> 0%
where the time goes in v1:
time: 182 us; the launch traced here: 181 us
  Pallas kernels  110 us (60%)
  matrix products  37.8 us (21%)
  starting transfers between devices  9.8 us (5%)
  waiting for transfers between devices  8.7 us (5%)
  other arithmetic  6.94 us (4%)
  local copies, waits for them, and re-layouts  6.27 us (3%)
    pallas_call x2, Pallas kernels, all_reduce(): pl.pallas_call(functools.partial(all_reduce_kernel, nslab, nsub), out_sha...  62.9 us
    pallas_call x1, Pallas kernels, subspace_bases(): pl.pallas_call(functools.partial(bases_kernel, 2), out_shape=(tall_shape,...  47.5 us
    dot_general x6, matrix products, tall(): lax.dot_general(first, second, (dims, ((), ())), precision=HIGH, preferre...  37.8 us
    ppermute x4, starting transfers between devices, shifted(): return lax.ppermute(face, axis, pairs)  9.8 us
    ppermute x4, waiting for transfers between devices, shifted(): return lax.ppermute(face, axis, pairs)  8.7 us
  transfers between devices with their start and end apart: 4, of which 1 were waited for; matrix products, arithmetic and copies ran while one was open for 7% of the time, Pallas kernels for 0%

profile of v1, /device:TPU:0, one launch (start us, length us, event | category | flops | bytes accessed | tf_op | source)
XLA Modules:
  0.0 181.3 jit_solution(18416723267616959670)
XLA Ops:
  0.6 19.1 %convolution_bitcast_fusion.in_ref = f32[512,512]{1,0:T(8,128)} fusion(f32[4,16,64,512]{3,2,1,0:T(8,128)} %param.7, f32[4,16,64,512]{3,2,1,0:T(8,128)} %param.8), kind=kOutput, calls=%fused_computation.14 | convolution fusion | flops 6442450944 | bytes 17825792 | tf_op jit(solution)/shard_map/dot_general | solution.py:22
  19.7 37.6 %shard_map.102.gram_ref = f32[2048,128]{1,0:T(8,128)} custom-call(f32[512,512]{1,0:T(8,128)} %convolution_bitcast_fusion.in_ref), custom_call_target="tpu_custom_call" | custom-call | tf_op jit(solution)/shard_map/pallas_call | solution.py:128
  57.3 47.5 %shard_map.103 = (f32[512,128]{1,0:T(8,128)}, f32[512,128]{1,0:T(8,128)}, f32[128,128]{1,0:T(8,128)}) custom-call(f32[2048,128]{1,0:T(8,128)} %shard_map.102.gram_ref, f32[512,128]{1,0:T(8,128)} %start_ref.1), custom_call_target="tpu_custom_call" | custom-call | tf_op jit(solution)/shard_map/pallas_call | solution.py:210
  104.8 7.8 %fusion.11 = f32[128,4096]{1,0:T(8,128)S(1)} fusion(f32[512,128]{1,0:T(8,128)} %get-tuple-element.9, f32[4096,512]{1,0:T(8,128)} %bitcast.39), kind=kOutput, calls=%fused_computation.26 | convolution fusion | flops 1610612736 | bytes 10747904 | tf_op jit(solution)/shard_map/dot_general | solution.py:22
  112.6 1.8 %copy.13 = f32[4096,128]{1,0:T(8,128)} copy(f32[4096,128]{0,1:T(8,128)S(1)} %bitcast.35) | data formatting | bytes 4194304 | tf_op jit(solution)/shard_map/dot_general | solution.py:22
  114.5 1.7 fusion.9
  116.1 2.3 %collective-permute-start.3 = (f32[4,1,64,128]{3,2,1,0:T(8,128)}, f32[4,1,64,128]{3,2,1,0:T(8,128)S(1)}, u32[]{:S(2)}, u32[]{:S(2)}) collective-permute-start(f32[4,1,64,128]{3,2,1,0:T(8,128)} %get-tuple-element.13), channel_id=1, source_target_pairs={{0,1},{1,2},{2,3},{4,5},{5,6},{6,7},{8,9},{9,10},{10,11},{12,13},{... | collective-permute-start | bytes 393224 | tf_op jit(solution)/shard_map/ppermute | solution.py:226
  118.4 0.0 copy-start.3
  118.4 1.4 collective-permute-start.2
  119.9 0.1 fusion.8
  120.0 1.0 copy.15
  121.0 4.8 %collective-permute-start.1 = (f32[1,16,64,128]{3,2,1,0:T(8,128)}, f32[1,16,64,128]{3,2,1,0:T(8,128)}, u32[]{:S(2)}, u32[]{:S(2)}) collective-permute-start(f32[1,16,64,128]{3,2,1,0:T(8,128)} %bitcast.42), channel_id=1, source_target_pairs={{0,4},{4,8},{8,12},{12,16},{16,20},{20,24},{24,28},{1,5},{5,9},{9,... | collective-permute-start | bytes 1572872 | tf_op jit(solution)/shard_map/ppermute | solution.py:226
  125.8 0.2 copy.14
  126.0 1.3 collective-permute-start
  127.3 0.9 copy.18
  128.2 0.0 copy-done.3
  128.2 7.7 %fusion.10 = f32[128,4096]{1,0:T(8,128)S(1)} fusion(f32[512,128]{1,0:T(8,128)S(1)} %copy-done.3, f32[4096,512]{1,0:T(8,128)} %bitcast.40), kind=kOutput, calls=%fused_computation.25 | convolution fusion | flops 1610612736 | bytes 10747904 | tf_op jit(solution)/shard_map/dot_general | solution.py:22
  135.9 0.0 copy-start
  135.9 0.0 copy-start.4
  136.0 0.0 copy-start.6
  136.0 0.9 convolution_bitcast_fusion.1
  136.9 0.0 copy-start.2
  136.9 0.0 copy-done.4
  136.9 0.1 copy.17
  137.0 0.3 copy-done
  137.3 0.9 convolution_bitcast_fusion.2
  138.2 0.0 copy-done.6
  138.2 0.1 mul.53
  138.9 0.1 pad.8.clone
  139.0 0.0 copy-start.1
  139.0 0.0 collective-permute-done.3
  139.0 0.0 collective-permute-done.2
  139.0 8.7 %collective-permute-done.1 = f32[1,16,64,128]{3,2,1,0:T(8,128)} collective-permute-done((f32[1,16,64,128]{3,2,1,0:T(8,128)}, f32[1,16,64,128]{3,2,1,0:T(8,128)}, u32[]{:S(2)}, u32[]{:S(2)}) %collective-permute-start.1) | collective-permute-done | bytes 524320 | tf_op jit(solution)/shard_map/ppermute | solution.py:226
  147.7 0.0 collective-permute-done
  147.7 0.0 copy-done.2
  147.7 3.3 %fusion.4 = f32[4,16,64,128]{3,2,1,0:T(8,128)S(1)} fusion(f32[4,16,64,128]{3,2,1,0:T(8,128)S(1)} %bitcast.38, f32[4,1,64,128]{3,2,1,0:T(8,128)S(1)} %collective-permute-done.3, f32[4,1,64,128]{3,2,1,0:T(8,128)} %collective-permute-done.2, f32[1,16,64,128]{3,2,1,0:T(8,128)} %collective-permute-done.1, f32[1,16,64,128]{3,2,1,0:T(8,128)S(1)} %collective-permute-done, ...), kind=kLoop, calls=%fused_computation.6 | loop fusion | flops 6815744 | bytes 5521408 | tf_op jit(solution)/shard_map/div | solution.py:254
  151.0 0.0 copy-done.1
  151.0 0.0 copy-start.5
  151.0 1.3 fusion.12
  152.3 0.8 maximum_maximum_fusion.in_ref
  153.1 25.3 %shard_map.104 = f32[256,128]{1,0:T(8,128)} custom-call(f32[256,128]{1,0:T(8,128)} %maximum_maximum_fusion.in_ref), custom_call_target="tpu_custom_call" | custom-call | tf_op jit(solution)/shard_map/pallas_call | solution.py:128
  178.4 1.3 slice_multiply_fusion
  179.8 0.0 copy-done.5
  179.8 1.6 multiply_multiply_fusion
  (2 shorter events, 0.0 us)
Async XLA Ops:
  116.1 22.9 %collective-permute-start.3 = (f32[4,1,64,128]{3,2,1,0:T(8,128)}, f32[4,1,64,128]{3,2,1,0:T(8,128)S(1)}, u32[]{:S(2)}, u32[]{:S(2)}) collective-permute-start(f32[4,1,64,128]{3,2,1,0:T(8,128)} %get-tuple-element.13), channel_id=1, source_target_pairs={{0,1},{1,2},{2,3},{4,5},{5,6},{6,7},{8,9},{9,10},{10,11},{12,13},{... | collective-permute-start | bytes 393224 | tf_op jit(solution)/shard_map/ppermute | solution.py:226
  118.4 9.8 %copy-start.3 = (f32[512,128]{1,0:T(8,128)S(1)}, f32[512,128]{1,0:T(8,128)}, u32[]{:S(2)}) copy-start(f32[512,128]{1,0:T(8,128)} %get-tuple-element.8) | copy-start | bytes 786436
  118.4 20.6 %collective-permute-start.2 = (f32[4,1,64,128]{3,2,1,0:T(8,128)}, f32[4,1,64,128]{3,2,1,0:T(8,128)}, u32[]{:S(2)}, u32[]{:S(2)}) collective-permute-start(f32[4,1,64,128]{3,2,1,0:T(8,128)} %get-tuple-element.12), channel_id=1, source_target_pairs={{1,0},{2,1},{3,2},{5,4},{6,5},{7,6},{9,8},{10,9},{11,10},{13,12},{... | collective-permute-start | bytes 393224 | tf_op jit(solution)/shard_map/ppermute | solution.py:226
  121.0 26.7 %collective-permute-start.1 = (f32[1,16,64,128]{3,2,1,0:T(8,128)}, f32[1,16,64,128]{3,2,1,0:T(8,128)}, u32[]{:S(2)}, u32[]{:S(2)}) collective-permute-start(f32[1,16,64,128]{3,2,1,0:T(8,128)} %bitcast.42), channel_id=1, source_target_pairs={{0,4},{4,8},{8,12},{12,16},{16,20},{20,24},{24,28},{1,5},{5,9},{9,... | collective-permute-start | bytes 1572872 | tf_op jit(solution)/shard_map/ppermute | solution.py:226
  126.0 21.7 %collective-permute-start = (f32[1,16,64,128]{3,2,1,0:T(8,128)S(1)}, f32[1,16,64,128]{3,2,1,0:T(8,128)S(1)}, u32[]{:S(2)}, u32[]{:S(2)}) collective-permute-start(f32[1,16,64,128]{3,2,1,0:T(8,128)S(1)} %bitcast.43), channel_id=1, source_target_pairs={{4,0},{8,4},{12,8},{16,12},{20,16},{24,20},{28,24},{5,1},{9,5},{13... | collective-permute-start | bytes 1572872 | tf_op jit(solution)/shard_map/ppermute | solution.py:226
  135.9 1.3 copy-start
  135.9 0.9 copy-start.4
  136.0 2.2 %copy-start.6 = (f32[4,1024]{1,0:T(4,128)S(1)}, f32[4,1024]{1,0:T(4,128)}, u32[]{:S(2)}) copy-start(f32[4,1024]{1,0:T(4,128)} %param.9) | copy-start | bytes 49156
  136.9 10.8 %copy-start.2 = (f32[4096,128]{1,0:T(8,128)S(1)}, f32[4096,128]{1,0:T(8,128)}, u32[]{:S(2)}) copy-start(f32[4096,128]{1,0:T(8,128)} %copy.13) | copy-start | bytes 6291460
  139.0 12.0 %copy-start.1 = (f32[128,4096]{1,0:T(8,128)S(1)}, f32[128,4096]{1,0:T(8,128)}, u32[]{:S(2)}) copy-start(f32[128,4096]{1,0:T(8,128)} %copy-done) | copy-start | bytes 6291460
  151.0 28.8 %copy-start.5 = (f32[128,128]{1,0:T(8,128)S(1)}, f32[128,128]{1,0:T(8,128)}, u32[]{:S(2)}) copy-start(f32[128,128]{1,0:T(8,128)} %get-tuple-element.7) | copy-start | bytes 196612

commit v2 on v1

--- a/solution.py
+++ b/solution.py
@@ -22,6 +22,52 @@
     return lax.dot_general(
         first, second, (dims, ((), ())), precision=HIGH, preferred_element_type=jnp.float32
     )
+
+
+def narrow(first, second, dims=((1,), (0,))):
+    return lax.dot_general(first, second, (dims, ((), ())), preferred_element_type=jnp.float32)
+
+
+def three_parts(value):
+    high = value.astype(jnp.bfloat16).astype(jnp.float32)
+    mid = (value - high).astype(jnp.bfloat16).astype(jnp.float32)
+    return high, mid, value - high - mid
+
+
+def two_parts(value):
+    high = value.astype(jnp.bfloat16)
+    return high, (value - high.astype(jnp.float32)).astype(jnp.bfloat16)
+
+
+def three_dots(first, second, dims=((1,), (0,))):
+    (a, b), (c, d) = two_parts(first), two_parts(second)
+    return narrow(a, c, dims) + (narrow(a, d, dims) + narrow(b, c, dims))
+
+
+def gram_kernel(first_ref, second_ref, out_ref):
+    @pl.when(pl.program_id(0) == 0)
+    def _():
+        out_ref[...] = jnp.zeros_like(out_ref)
+
+    out_ref[...] += three_dots(first_ref[...], second_ref[...], ((0,), (0,)))
+
+
+def cells_step(cells):
+    return 512 if cells % 512 == 0 else cells
+
+
+def gram(first, second):
+    cells, wide = first.shape
+    step = cells_step(cells)
+    spec = pl.BlockSpec((step, wide), lambda k: (k, 0))
+    return pl.pallas_call(
+        gram_kernel,
+        grid=(cells // step,),
+        out_shape=jax.ShapeDtypeStruct((wide, second.shape[1]), jnp.float32),
+        in_specs=[spec, spec],
+        out_specs=pl.BlockSpec((wide, second.shape[1]), lambda k: (0, 0)),
+        compiler_params=pltpu.CompilerParams(dimension_semantics=("arbitrary",)),
+    )(first, second)
 
 
 def sub_bits(count):
@@ -135,6 +181,88 @@
             pltpu.VMEM((rows, LANES), jnp.float32),
             pltpu.VMEM((nslab, piece, LANES), jnp.float32),
             sub_sem, sub_sem, slab_sem, slab_sem, slab_sem, slab_sem, sub_sem, sub_sem,
+        ],
+        compiler_params=pltpu.CompilerParams(collective_id=ident, has_side_effects=True),
+    )(part)
+
+
+def small_kernel(nslab, nsub, in_ref, out_ref, total, slots, got_slab, *sems):
+    sub_send, sub_recv, rs_send, rs_recv, ag_send, ag_recv = sems
+    slab, sub = lax.axis_index("slab"), lax.axis_index("sub")
+    barrier = pltpu.get_barrier_semaphore()
+    for off in range(1, nsub):
+        pl.semaphore_signal(barrier, inc=1, device_id={"sub": lax.rem(sub + off, nsub)})
+    for off in range(1, nslab):
+        pl.semaphore_signal(barrier, inc=1, device_id={"slab": lax.rem(slab + off, nslab)})
+    pl.semaphore_wait(barrier, nsub + nslab - 2)
+
+    copies = []
+    for off in range(1, nsub):
+        copy = pltpu.make_async_remote_copy(
+            src_ref=in_ref,
+            dst_ref=slots.at[sub],
+            send_sem=sub_send.at[off],
+            recv_sem=sub_recv.at[off],
+            device_id={"sub": lax.rem(sub + off, nsub)},
+        )
+        copy.start()
+        copies.append(copy)
+    slots[sub] = in_ref[...]
+    for copy in copies:
+        copy.wait()
+    value = slots[0]
+    for k in range(1, nsub):
+        value = value + slots[k]
+    total[...] = value
+
+    piece = in_ref.shape[0] // nslab
+    copies = []
+    for off in range(1, nslab):
+        peer = lax.rem(slab + off, nslab)
+        copy = pltpu.make_async_remote_copy(
+            src_ref=total.at[pl.ds(pl.multiple_of(peer * piece, 8), piece)],
+            dst_ref=got_slab.at[off],
+            send_sem=rs_send.at[off],
+            recv_sem=rs_recv.at[off],
+            device_id={"slab": peer},
+        )
+        copy.start()
+        copies.append(copy)
+    mine = pl.multiple_of(slab * piece, 8)
+    value = total[pl.ds(mine, piece), :]
+    for off in range(1, nslab):
+        copies[off - 1].wait()
+        value = value + got_slab[off]
+    out_ref[pl.ds(mine, piece), :] = value
+    copies = []
+    for off in range(1, nslab):
+        copy = pltpu.make_async_remote_copy(
+            src_ref=out_ref.at[pl.ds(mine, piece)],
+            dst_ref=out_ref.at[pl.ds(mine, piece)],
+            send_sem=ag_send.at[off],
+            recv_sem=ag_recv.at[off],
+            device_id={"slab": lax.rem(slab + off, nslab)},
+        )
+        copy.start()
+        copies.append(copy)
+    for copy in copies:
+        copy.wait()
+
+
+def small_all_reduce(part, ident):
+    nslab, nsub = lax.axis_size("slab"), lax.axis_size("sub")
+    rows = part.shape[0]
+    sub_sem, slab_sem = pltpu.SemaphoreType.DMA((nsub,)), pltpu.SemaphoreType.DMA((nslab,))
+    return pl.pallas_call(
+        functools.partial(small_kernel, nslab, nsub),
+        out_shape=jax.ShapeDtypeStruct((rows, LANES), jnp.float32),
+        in_specs=[pl.BlockSpec(memory_space=pltpu.VMEM)],
+        out_specs=pl.BlockSpec(memory_space=pltpu.VMEM),
+        scratch_shapes=[
+            pltpu.VMEM((rows, LANES), jnp.float32),
+            pltpu.VMEM((nsub, rows, LANES), jnp.float32),
+            pltpu.VMEM((nslab, rows // nslab, LANES), jnp.float32),
+            sub_sem, sub_sem, slab_sem, slab_sem, slab_sem, slab_sem,
         ],
         compiler_params=pltpu.CompilerParams(collective_id=ident, has_side_effects=True),
     )(part)
@@ -170,8 +298,10 @@
             panel = jnp.where(place == i, rows[i], panel)
         work[base : base + PANEL, :] = panel
         if base + PANEL < size:
-            left = panel[:, :size]
-            update = exact(left, panel, ((0,), (0,)))
+            high, mid, low = three_parts(panel)
+            first = jnp.concatenate([high, high, mid, high, low, mid], axis=0)[:, :size]
+            second = jnp.concatenate([high, mid, high, low, high, mid], axis=0)
+            update = narrow(first.astype(jnp.bfloat16), second.astype(jnp.bfloat16), ((0,), (0,)))
             work[base + PANEL :, :] = work[base + PANEL :, :] - update[base + PANEL :, :]
 
 
@@ -220,10 +350,141 @@
     )(cross_gram, start_block)
 
 
-def shifted(face, axis, step):
-    count = lax.axis_size(axis)
-    pairs = [(i, i + step) for i in range(count) if 0 <= i + step < count]
-    return lax.ppermute(face, axis, pairs)
+def block_order(k, count, per_plane):
+    inner = jnp.where(k < 2 * per_plane, count - 2 * per_plane + k, k - per_plane)
+    return jnp.where(k < per_plane, k, inner)
+
+
+def project_kernel(nslab, nsub, per_plane, *refs):
+    ctrl_cells, obs_cells, right_ref, left_ref, ctrl_ref, obs_ref = refs[:6]
+    faces, halves, landed, (send, recv) = refs[6:10], refs[10], refs[11:15], refs[15:]
+    k = pl.program_id(0)
+    count = pl.num_programs(0) // 2
+    planes, lines, points, size = ctrl_ref.shape
+    slab, sub = lax.axis_index("slab"), lax.axis_index("sub")
+    moves = (
+        ("slab", slab, nslab, 1, ctrl_ref.at[planes - 1]),
+        ("slab", slab, nslab, -1, ctrl_ref.at[0]),
+        ("sub", sub, nsub, 1, ctrl_ref.at[:, lines - 1]),
+        ("sub", sub, nsub, -1, ctrl_ref.at[:, 0]),
+    )
+
+    def there(me, total, step):
+        return me < total - 1 if step > 0 else me > 0
+
+    def copy(m):
+        axis, me, _, step, source = moves[m]
+        return pltpu.make_async_remote_copy(
+            src_ref=source,
+            dst_ref=landed[m],
+            send_sem=send.at[m],
+            recv_sem=recv.at[m],
+            device_id={axis: me + step},
+        )
+
+    def each(picked, act):
+        for m in picked:
+            _, me, total, step, _ = moves[m]
+
+            @pl.when(there(me, total, step))
+            def _():
+                act(m)
+
+    def product(cells, which):
+        high, low = two_parts(cells)
+        wide = narrow(high, halves[which])
+        return wide[:, :size] + (wide[:, size:] + narrow(low, halves[which, :, :size]))
+
+    @pl.when(k == 0)
+    def _():
+        barrier = pltpu.get_barrier_semaphore()
+        for axis, me, total, step, _ in moves:
+            beside = lax.rem(me + step + total, total)
+            pl.semaphore_signal(barrier, inc=1, device_id={axis: beside})
+        pl.semaphore_wait(barrier, len(moves))
+        for which, basis in enumerate((right_ref, left_ref)):
+            high, low = two_parts(basis[...])
+            halves[which, :, :size] = high
+            halves[which, :, size:] = low
+
+    @pl.when(k < count)
+    def _():
+        block = block_order(k, count, per_plane)
+        some = lines // per_plane
+        value = product(ctrl_cells[...], 0).reshape(some, points, size)
+        ctrl_ref[block // per_plane, pl.ds(lax.rem(block, per_plane) * some, some)] = value
+
+    @pl.when(k >= count)
+    def _():
+        obs_ref[...] = product(obs_cells[...], 1)
+
+    @pl.when(k == 2 * per_plane - 1)
+    def _():
+        each((0, 1), lambda m: copy(m).start())
+
+    @pl.when(k == count - 1)
+    def _():
+        each((2, 3), lambda m: copy(m).start())
+
+    @pl.when(k == 2 * count - 1)
+    def _():
+        for m, (_, me, total, step, _) in enumerate(moves):
+
+            @pl.when(there(me, total, step))
+            def _():
+                copy(m).wait_send()
+
+            @pl.when(there(me, total, -step))
+            def _():
+                copy(m).wait_recv()
+                faces[m][...] = landed[m][...]
+
+            @pl.when(jnp.logical_not(there(me, total, -step)))
+            def _():
+                faces[m][...] = jnp.zeros(landed[m].shape, jnp.float32)
+
+
+def project(factor_ctrl, factor_obs, right_basis, left_basis, ident):
+    nslab, nsub = lax.axis_size("slab"), lax.axis_size("sub")
+    planes, lines, points, wide = factor_ctrl.shape
+    cells, size = planes * lines * points, right_basis.shape[1]
+    per_plane = 2 if lines % 2 == 0 else 1
+    count, step = planes * per_plane, lines * points // per_plane
+    shapes = [(lines, points, size)] * 2 + [(planes, points, size)] * 2
+    grid_shape = (planes, lines, points, size)
+    four = pltpu.SemaphoreType.DMA((4,))
+    basis_spec = pl.BlockSpec((wide, size), lambda k: (0, 0))
+    return pl.pallas_call(
+        functools.partial(project_kernel, nslab, nsub, per_plane),
+        grid=(2 * count,),
+        out_shape=[
+            jax.ShapeDtypeStruct(grid_shape, jnp.float32),
+            jax.ShapeDtypeStruct((cells, size), jnp.float32),
+        ]
+        + [jax.ShapeDtypeStruct(shape, jnp.float32) for shape in shapes],
+        in_specs=[
+            pl.BlockSpec(
+                (step, wide),
+                lambda k: (block_order(jnp.minimum(k, count - 1), count, per_plane), 0),
+            ),
+            pl.BlockSpec((step, wide), lambda k: (jnp.maximum(k - count, 0), 0)),
+            basis_spec,
+            basis_spec,
+        ],
+        out_specs=[
+            pl.BlockSpec(grid_shape, lambda k: (0, 0, 0, 0)),
+            pl.BlockSpec((step, size), lambda k: (jnp.maximum(k - count, 0), 0)),
+        ]
+        + [pl.BlockSpec(shape, lambda k: (0, 0, 0)) for shape in shapes],
+        scratch_shapes=[pltpu.VMEM((2, wide, 2 * size), jnp.bfloat16)]
+        + [pltpu.VMEM(shape, jnp.float32) for shape in shapes]
+        + [four, four],
+        compiler_params=pltpu.CompilerParams(
+            collective_id=ident,
+            has_side_effects=True,
+            dimension_semantics=("arbitrary",),
+        ),
+    )(factor_ctrl.reshape(cells, wide), factor_obs.reshape(cells, wide), right_basis, left_basis)
 
 
 def on_device(factor_obs, factor_ctrl, diffusivity, input_map, output_map, start_block, order):
@@ -237,16 +498,15 @@
     sense = output_map.reshape(output_map.shape[0], cells)
     ins, outs = drive.shape[0], sense.shape[0]
 
-    cross_gram = all_reduce(tall(observe, control, ((0,), (0,))), 0)
+    cross_gram = all_reduce(gram(observe, control), 0)
     left_basis, right_basis, mass = subspace_bases(cross_gram, start_block)
 
-    ctrl_flat = tall(control, right_basis)
-    ctrl = ctrl_flat.reshape(planes, lines, points, size)
-    below = shifted(ctrl[-1:], "slab", 1)
-    above = shifted(ctrl[:1], "slab", -1)
-    before = shifted(ctrl[:, -1:], "sub", 1)
-    after = shifted(ctrl[:, :1], "sub", -1)
-    obs_space = tall(observe, left_basis)
+    ctrl, obs_space, below, above, before, after = project(
+        factor_ctrl, factor_obs, right_basis, left_basis, 2
+    )
+    ctrl_flat = ctrl.reshape(cells, size)
+    below, above = below[None], above[None]
+    before, after = before[:, None], after[:, None]
     zs = jnp.concatenate([below, ctrl, above], axis=0)
     ys = jnp.concatenate([before, ctrl, after], axis=1)
     xs = jnp.pad(ctrl, ((0, 0), (0, 0), (1, 1), (0, 0)))
@@ -254,7 +514,7 @@
     applied = (conduct[..., None] * (beside - 6.0 * ctrl) / 6.0).reshape(cells, size)
     state = tall(obs_space, applied, ((0,), (0,)))
     used = size + ins + outs
-    grain = 8 * lax.axis_size("slab") * lax.axis_size("sub")
+    grain = 8 * lax.axis_size("slab")
     packed = jnp.concatenate(
         [
             state,
@@ -264,7 +524,7 @@
         ],
         axis=0,
     )
-    summed = all_reduce(packed, 1)
+    summed = small_all_reduce(packed, 1)
     kept = (jnp.arange(size, dtype=jnp.int32) < order[0]).astype(jnp.float32)
     square = kept[:, None] * kept[None, :]
     reduced_input = kept[:, None] * summed[size : size + ins].T

time: 182 us -> 156 us (0.86)
  matrix products: 37.8 us -> 3.13 us
  Pallas kernels: 110 us -> 139 us
  starting transfers between devices: 9.8 us -> 0 us
  waiting for transfers between devices: 8.7 us -> 0 us
  local copies, waits for them, and re-layouts: 6.27 us -> 0.42 us
  other arithmetic: 6.94 us -> 11.1 us
    pallas_call x0 -> x3, Pallas kernels: none -> 66.6 us  [the longest x1 33.1 us: project(): pl.pallas_call(functools.partial(project_kernel, nslab, nsub, per_plane),...]
    dot_general x6 -> x3, matrix products: 37.8 us -> 3.13 us  [tall(): lax.dot_general(first, second, (dims, ((), ())), precision=HIGH, preferre...]
    pallas_call x2 -> x1, Pallas kernels: 62.9 us -> 37.6 us  [all_reduce(): pl.pallas_call(functools.partial(all_reduce_kernel, nslab, nsub), out_sha...]
    pallas_call x1, Pallas kernels: 47.5 us -> 35 us  [subspace_bases(): pl.pallas_call(functools.partial(bases_kernel, 2), out_shape=(tall_shape,...]
    ppermute x4 -> x0, starting transfers between devices: 9.8 us -> none  [shifted(): return lax.ppermute(face, axis, pairs)]
    ppermute x4 -> x0, waiting for transfers between devices: 8.7 us -> none  [shifted(): return lax.ppermute(face, axis, pairs)]
    div x1, other arithmetic: 3.26 us -> 7.43 us  [on_device(): conduct[..., None] * (beside - 6.0 * ctrl) / 6.0]
    slice x4 -> x0, local copies, waits for them, and re-layouts: 2.98 us -> none  [the longest x1 1.69 us: on_device(): after = shifted(ctrl[:, :1], 'sub', -1)]
  transfers between devices with their start and end apart: 4 -> 0, of which waited for: 1 -> 0; matrix products, arithmetic and copies ran while one was open for 7% -> 0% of each run, Pallas kernels for 0% -> 0%
where the time goes in v2:
time: 156 us; the launch traced here: 155 us
  Pallas kernels  139 us (89%)
  other arithmetic  11.1 us (7%)
  matrix products  3.13 us (2%)
    pallas_call x1, Pallas kernels, all_reduce(): pl.pallas_call(functools.partial(all_reduce_kernel, nslab, nsub), out_sha...  37.6 us
    pallas_call x1, Pallas kernels, subspace_bases(): pl.pallas_call(functools.partial(bases_kernel, 2), out_shape=(tall_shape,...  35 us
    pallas_call x1, Pallas kernels, project(): pl.pallas_call(functools.partial(project_kernel, nslab, nsub, per_plane),...  33.1 us
    pallas_call x1, Pallas kernels, small_all_reduce(): pl.pallas_call(functools.partial(small_kernel, nslab, nsub), out_shape=ja...  20.7 us
    pallas_call x1, Pallas kernels, gram(): pl.pallas_call(gram_kernel, grid=(cells // step,), out_shape=jax.ShapeDty...  12.7 us
    div x1, other arithmetic, on_device(): conduct[..., None] * (beside - 6.0 * ctrl) / 6.0  7.43 us
    dot_general x3, matrix products, tall(): lax.dot_general(first, second, (dims, ((), ())), precision=HIGH, preferre...  3.13 us

profile of v2, /device:TPU:0, one launch (start us, length us, event | category | flops | bytes accessed | tf_op | source)
XLA Modules:
  0.0 155.2 jit_solution(2652333956970895507)
XLA Ops:
  0.6 12.7 %shard_map.102.in_ref = f32[512,512]{1,0:T(8,128)} custom-call(f32[4096,512]{1,0:T(8,128)} %bitcast.32, f32[4096,512]{1,0:T(8,128)} %bitcast.30), custom_call_target="tpu_custom_call" | custom-call | tf_op jit(solution)/shard_map/pallas_call | solution.py:63
  13.4 37.6 %shard_map.103.gram_ref = f32[2048,128]{1,0:T(8,128)} custom-call(f32[512,512]{1,0:T(8,128)} %shard_map.102.in_ref), custom_call_target="tpu_custom_call" | custom-call | tf_op jit(solution)/shard_map/pallas_call | solution.py:174
  50.9 35.0 %shard_map.104 = (f32[512,128]{1,0:T(8,128)}, f32[512,128]{1,0:T(8,128)}, f32[128,128]{1,0:T(8,128)}) custom-call(f32[2048,128]{1,0:T(8,128)} %shard_map.103.gram_ref, f32[512,128]{1,0:T(8,128)} %start_ref.1), custom_call_target="tpu_custom_call" | custom-call | tf_op jit(solution)/shard_map/pallas_call | solution.py:340
  85.9 0.0 copy-start.5
  85.9 33.1 %shard_map.105 = (f32[4,16,64,128]{3,2,1,0:T(8,128)}, f32[4096,128]{1,0:T(8,128)}, f32[16,64,128]{2,1,0:T(8,128)}, f32[16,64,128]{2,1,0:T(8,128)}, f32[4,64,128]{2,1,0:T(8,128)}, /*index=5*/f32[4,64,128]{2,1,0:T(8,128)}) custom-call(f32[4096,512]{1,0:T(8,128)} %bitcast.31, f32[4096,512]{1,0:T(8,128)} %bitcast.33, f32[512,128]{1,0:T(8,128)} %get-tuple-element.14.refs_2_, ...), custom_call_target="tpu_custom_call" | custom-call | tf_op jit(solution)/shard_map/pallas_call | solution.py:457
  119.1 0.0 copy-done.5
  119.1 0.1 mul.53
  119.1 0.0 copy-start
  119.2 7.4 %fusion.4 = f32[4,16,64,128]{3,2,1,0:T(8,128)S(1)} fusion(f32[4,16,64,128]{3,2,1,0:T(8,128)} %get-tuple-element.17, f32[4,1,64,128]{3,2,1,0:T(8,128)} %bitcast.40, f32[4,1,64,128]{3,2,1,0:T(8,128)} %bitcast.41, f32[1,16,64,128]{3,2,1,0:T(8,128)} %bitcast.36, f32[1,16,64,128]{3,2,1,0:T(8,128)} %bitcast.37, f32[4,16,64]{2,1,0:T(8,128)S(1)} %mul.53), kind=kLoop, calls=%fused_computation.6 | loop fusion | flops 6815744 | bytes 5521408 | tf_op jit(solution)/shard_map/div | solution.py:514
  126.6 0.0 copy-done
  126.6 0.0 copy-start.2
  126.6 0.0 copy-start.1
  126.6 1.9 %fusion.8 = f32[128,128]{1,0:T(8,128)S(1)} fusion(f32[4096,128]{1,0:T(8,128)S(1)} %copy-done, f32[4096,128]{1,0:T(8,128)S(1)} %bitcast.35), kind=kOutput, calls=%fused_computation.22 | convolution fusion | flops 402653184 | bytes 4259840 | tf_op jit(solution)/shard_map/dot_general | solution.py:22
  128.5 0.0 copy-start.3
  128.6 0.0 copy-done.2
  128.6 0.0 copy-done.1
  128.6 0.0 copy-start.4
  128.6 0.6 convolution_bitcast_fusion
  129.2 0.1 copy-done.3
  129.4 0.6 convolution_bitcast_fusion.1
  130.0 0.1 pad.8.clone
  130.1 0.7 maximum_maximum_fusion.in_ref
  130.9 20.7 %shard_map.106 = f32[192,128]{1,0:T(8,128)} custom-call(f32[192,128]{1,0:T(8,128)} %maximum_maximum_fusion.in_ref), custom_call_target="tpu_custom_call" | custom-call | tf_op jit(solution)/shard_map/pallas_call | solution.py:256
  152.3 0.0 copy-done.4
  152.3 1.6 %multiply_multiply_fusion = (f32[128,128]{1,0:T(8,128)}, f32[128,128]{1,0:T(8,128)}) fusion(f32[192,128]{1,0:T(8,128)} %shard_map.106, f32[128]{0:T(128)S(1)} %compare_convert_fusion, f32[128,128]{1,0:T(8,128)S(1)} %copy-done.4), kind=kLoop, calls=%fused_computation.17 | loop fusion | flops 49152 | bytes 263168 | tf_op jit(solution)/shard_map/mul | solution.py:532
  153.9 1.3 slice_multiply_fusion
  (4 shorter events, 0.1 us)
Async XLA Ops:
  85.9 33.2 %copy-start.5 = (f32[4,1024]{1,0:T(4,128)S(1)}, f32[4,1024]{1,0:T(4,128)}, u32[]{:S(2)}) copy-start(f32[4,1024]{1,0:T(4,128)} %param.9) | copy-start | bytes 49156
  119.1 7.4 %copy-start = (f32[4096,128]{1,0:T(8,128)S(1)}, f32[4096,128]{1,0:T(8,128)}, u32[]{:S(2)}) copy-start(f32[4096,128]{1,0:T(8,128)} %get-tuple-element.16) | copy-start | bytes 6291460
  126.6 2.0 %copy-start.2 = (f32[4,4,1024]{2,1,0:T(4,128)S(1)}, f32[4,4,1024]{2,1,0:T(4,128)}, u32[]{:S(2)}) copy-start(f32[4,4,1024]{2,1,0:T(4,128)} %param.11) | copy-start | bytes 196612
  126.6 2.0 %copy-start.1 = (f32[4,16,64,128]{3,2,1,0:T(8,128)S(1)}, f32[4,16,64,128]{3,2,1,0:T(8,128)}, u32[]{:S(2)}) copy-start(f32[4,16,64,128]{3,2,1,0:T(8,128)} %get-tuple-element.17) | copy-start | bytes 6291460
  128.5 0.8 copy-start.3
  128.6 23.6 %copy-start.4 = (f32[128,128]{1,0:T(8,128)S(1)}, f32[128,128]{1,0:T(8,128)}, u32[]{:S(2)}) copy-start(f32[128,128]{1,0:T(8,128)} %get-tuple-element.13) | copy-start | bytes 196612
